TPU v7x, 32 devices: a whole 2x2x4 slice. The times are simulated.
32 devices in a mesh: slab: 4 (over x, core), rep: 8 (over z, y).
Axes of the slice: x: 2, y: 2, z: 4, core: 2. Of those that a mesh axis runs over, the one named last changes fastest.
Arguments:
- image: float32 [144, 256, 256], P('slab', 'rep'), may hold values from 0.5 to 2
- sensitivity: float32 [144, 256, 256], P('slab', 'rep'), may hold values from 0.5 to 2
- system_blocks: bfloat16 [512, 128, 1024], P(('slab', 'rep')), may hold values from 0 to 0.00390625
- tile_slab: int32 [512, 1], P(('slab', 'rep')), may hold values from 0 to 3; in each aligned block of 16 rows (0 to 15, 16 to 31, ...) at most 6 rows name the same one
- tile_block: int32 [512], P(('slab', 'rep')), may hold values from 0 to 2303
- background: bfloat16 [512, 128], P(('slab', 'rep')), may hold values from 0.19921875 to 1
Outputs:
- updated: float32 [144, 256, 256], P('slab', 'rep')
Inputs may be any that keep to these rules, and one draw needn't show every extreme that they name: `tile_slab`: among the 16 tiles of one device at most 6 view the same slab, and in some devices some slab is viewed by exactly 6.
All inputs are finite; a program needn't handle non-finite values.
Results may differ from a plain program's by a relative error of at most 0.0003.
Values may be sent and summed in bfloat16 or wider, within the bound.
No kernel may reach another device: no remote copies, remote signals or barrier semaphores. Data moves between devices by JAX's collectives and lax.ppermute only.
A program may use at most 64 MiB of HBM per device.

v0:
```python
import jax
import jax.numpy as jnp
from jax import lax
from jax.sharding import PartitionSpec as P

CAP = 6


def local(image, sensitivity, system_blocks, tile_slab, tile_block, background):
    slab_count = lax.axis_size("slab")
    tiles_here, tile_rows, width = system_blocks.shape
    destination = tile_slab[:, 0]
    replica_total = lax.axis_size("rep")
    detector_plane_count, local_rows, column_count = image.shape
    local_blocks = image.astype(jnp.bfloat16).reshape(-1, width)
    per_plane = local_rows * replica_total * column_count // width
    per_owner = local_rows * column_count // width
    within = tile_block % per_plane
    plane_of = tile_block // per_plane
    owner_rep = within // per_owner
    local_id = plane_of * per_owner + within % per_owner
    key = destination * replica_total + owner_rep
    key_hot = (
        key[:, None] == jnp.arange(slab_count * replica_total, dtype=jnp.int32)[None, :]
    ).astype(jnp.int32)
    position_order = jnp.sum((jnp.cumsum(key_hot, axis=0) - key_hot) * key_hot, axis=1)
    id_buffer = (
        jnp.zeros((slab_count, replica_total, CAP), jnp.int32)
        .at[destination, owner_rep, position_order]
        .set(local_id)
    )
    asked = lax.all_to_all(
        lax.all_to_all(id_buffer, "slab", split_axis=0, concat_axis=0, tiled=True),
        "rep",
        split_axis=1,
        concat_axis=1,
        tiled=True,
    )
    served_requests = local_blocks[asked]
    returned = lax.all_to_all(
        lax.all_to_all(served_requests, "slab", split_axis=0, concat_axis=0, tiled=True),
        "rep",
        split_axis=1,
        concat_axis=1,
        tiled=True,
    )
    emission_cell_entries = returned[destination, owner_rep, position_order]
    forward_projection = jnp.einsum(
        "tev,tv->te", system_blocks, emission_cell_entries, preferred_element_type=jnp.float32
    )
    inverse_permutation = (1.0 / (forward_projection + background.astype(jnp.float32))).astype(
        jnp.bfloat16
    )
    own_back = jnp.einsum(
        "tev,te->tv", system_blocks, inverse_permutation, preferred_element_type=jnp.float32
    )
    back_buffer = (
        jnp.zeros((slab_count, replica_total, CAP, width), jnp.float32)
        .at[destination, owner_rep, position_order]
        .set(own_back)
    )
    received_tiles = lax.all_to_all(
        lax.all_to_all(back_buffer, "slab", split_axis=0, concat_axis=0, tiled=True),
        "rep",
        split_axis=1,
        concat_axis=1,
        tiled=True,
    )
    owned = (
        jnp.zeros(local_blocks.shape, jnp.float32)
        .at[asked.reshape(-1)]
        .add(received_tiles.reshape(-1, width))
    )
    return image * owned.reshape(image.shape) / sensitivity


def solution(mesh):
    return jax.shard_map(
        local,
        mesh=mesh,
        in_specs=(
            P("slab", "rep", None),
            P("slab", "rep", None),
            P(("slab", "rep"), None, None),
            P(("slab", "rep"), None),
            P(("slab", "rep")),
            P(("slab", "rep"), None),
        ),
        out_specs=P("slab", "rep", None),
        check_vma=False,
    )
```

profile of v0, /device:TPU:0, one launch (start us, length us, event | category | flops | bytes accessed | tf_op | source)
XLA Modules:
  0.0 104.5 jit_solution(2315465785091688998)
XLA Ops:
  0.0 0.8 fusion.8
  0.8 0.7 bitcast_add_fusion
  1.6 0.2 select_reduce_fusion
  1.7 0.7 fusion.12
  2.4 1.5 %scatter_fusion = s32[4,8,6]{1,0,2:T(4,128)S(1)} fusion(s32[4,8,6]{1,0,2:T(4,128)S(1)} %broadcast.74, s32[16]{0:T(128)S(1)} %get-tuple-element.8, s32[16]{0:T(128)S(1)} %get-tuple-element.5), kind=kCustom, calls=%fused_computation.2 | custom fusion | bytes 384 | tf_op jit(solution)/shard_map/scatter | solution.py:30
  3.9 7.9 %all_to_all.30 = s32[4,8,6]{1,2,0:T(8,128)S(1)} all-to-all(s32[4,8,6]{1,2,0:T(8,128)S(1)} %copy.23), channel_id=1, replica_groups=mesh['slab'=4,'rep'=8] {'slab'}, dimensions={0} | all-to-all | bytes 1536 | tf_op jit(solution)/shard_map/all_to_all | solution.py:33
  11.8 0.7 copy.24
  12.5 5.8 %all-to-all-start.1 = ((s32[4,8,6]{2,0,1:T(4,128)}), s32[4,8,6]{2,0,1:T(4,128)S(1)}, u32[]{:S(2)}, u32[]{:S(2)}) async-start(s32[4,8,6]{2,0,1:T(4,128)} %copy.24), calls=%async_computation.1 | async-start | bytes 32768 | tf_op jit(solution)/shard_map/all_to_all | solution.py:32
  18.5 0.4 reshape.57
  18.8 6.1 %all-to-all-done.1 = s32[4,8,6]{2,0,1:T(4,128)S(1)} async-done(((s32[4,8,6]{2,0,1:T(4,128)}), s32[4,8,6]{2,0,1:T(4,128)S(1)}, u32[]{:S(2)}, u32[]{:S(2)}) %all-to-all-start.1) | async-done | bytes 800 | tf_op jit(solution)/shard_map/all_to_all | solution.py:32
  24.9 0.1 copy.26
  25.1 0.1 copy.29
  25.3 1.0 gather_fusion
  26.3 0.1 reshape.61
  26.4 0.2 copy.30
  26.7 9.8 %all_to_all.31 = bf16[4,8,6,1024]{3,1,2,0:T(8,128)(2,1)S(1)} all-to-all(bf16[4,8,6,1024]{3,1,2,0:T(8,128)(2,1)S(1)} %copy.30), channel_id=1, replica_groups=mesh['slab'=4,'rep'=8] {'slab'}, dimensions={0} | all-to-all | bytes 786432 | tf_op jit(solution)/shard_map/all_to_all | solution.py:41
  36.5 0.3 copy.31
  36.8 14.4 %all_to_all.32 = bf16[4,8,6,1024]{3,0,2,1:T(4,128)(2,1)S(1)} all-to-all(bf16[4,8,6,1024]{3,0,2,1:T(4,128)(2,1)S(1)} %copy.31), channel_id=1, replica_groups=mesh['slab'=4,'rep'=8] {'rep'}, dimensions={1} | all-to-all | bytes 786432 | tf_op jit(solution)/shard_map/all_to_all | solution.py:40
  51.2 0.2 copy.32
  51.4 0.7 gather_fusion.1
  52.1 3.5 %fusion.2 = f32[16,1,128]{2,1,0:T(1,128)S(1)} fusion(bf16[16,128,1024]{2,1,0:T(8,128)(2,1)} %param.8, bf16[16,1024,1]{1,0,2:T(8,128)(2,1)S(1)} %bitcast.32), kind=kOutput, calls=%fused_computation.9 | convolution fusion | flops 4194304 | bytes 4235264 | tf_op jit(solution)/shard_map/tev,tv->te/dot_general | solution.py:48
  55.7 0.7 fusion.4
  56.4 1.6 %scatter_fusion.1 = f32[4,8,6,1024]{3,1,2,0:T(8,128)S(1)} fusion(f32[4,8,6,1024]{3,1,2,0:T(8,128)S(1)} %broadcast_in_dim.10, s32[16]{0:T(128)S(1)} %get-tuple-element.8, f32[16,1024]{1,0:T(8,128)S(1)} %bitcast.33), kind=kCustom, calls=%fused_computation.3 | custom fusion | bytes 196800 | tf_op jit(solution)/shard_map/scatter | solution.py:60
  58.0 14.0 %all_to_all.33 = f32[4,8,6,1024]{3,1,2,0:T(8,128)S(1)} all-to-all(f32[4,8,6,1024]{3,1,2,0:T(8,128)S(1)} %scatter_fusion.1), channel_id=1, replica_groups=mesh['slab'=4,'rep'=8] {'slab'}, dimensions={0} | all-to-all | bytes 1572864 | tf_op jit(solution)/shard_map/all_to_all | solution.py:63
  72.1 1.4 %copy.33 = f32[4,8,6,1024]{3,0,2,1:T(4,128)} copy(f32[4,8,6,1024]{3,1,2,0:T(8,128)S(1)} %all_to_all.33) | data formatting | bytes 1572864 | tf_op jit(solution)/shard_map/all_to_all | solution.py:63
  73.5 3.5 %all-to-all-start.5 = ((f32[4,8,6,1024]{3,0,2,1:T(4,128)}), f32[4,8,6,1024]{3,0,2,1:T(4,128)S(1)}, u32[]{:S(2)}, u32[]{:S(2)}) async-start(f32[4,8,6,1024]{3,0,2,1:T(4,128)} %copy.33), calls=%async_computation.5 | async-start | bytes 1572864 | tf_op jit(solution)/shard_map/all_to_all | solution.py:62
  77.2 19.9 %all-to-all-done.5 = f32[4,8,6,1024]{3,0,2,1:T(4,128)S(1)} async-done(((f32[4,8,6,1024]{3,0,2,1:T(4,128)}), f32[4,8,6,1024]{3,0,2,1:T(4,128)S(1)}, u32[]{:S(2)}, u32[]{:S(2)}) %all-to-all-start.5) | async-done | bytes 786464 | tf_op jit(solution)/shard_map/all_to_all | solution.py:62
  97.1 0.5 copy.34
  97.6 1.0 reshape.90
  98.6 3.0 %scatter_custom_fusion.2 = f32[288,1024]{1,0:T(8,128)S(1)} fusion(s32[192]{0:T(256)S(1)} %bitcast.36, f32[192,1024]{1,0:T(8,128)} %reshape.90, f32[]{:T(128)} %constant.55.clone.1), kind=kCustom, calls=%fused_computation.6 | custom fusion | flops 196608 | bytes 1180160 | tf_op jit(solution)/shard_map/scatter-add | solution.py:72
  101.6 0.3 reshape.59
  101.9 2.6 %multiply_divide_fusion = f32[36,32,256]{2,1,0:T(8,128)} fusion(f32[36,32,256]{2,1,0:T(8,128)} %param.7, f32[36,32,256]{2,1,0:T(8,128)S(1)} %copy-done.1, f32[36,32,256]{2,1,0:T(8,128)S(1)} %reshape.59), kind=kLoop, calls=%fused_computation.5 | loop fusion | flops 589824 | bytes 4718592 | tf_op jit(solution)/shard_map/div | solution.py:74
  (20 shorter events, 0.5 us)
Async XLA Ops:
  0.0 18.4 %copy-start.1 = (f32[36,32,256]{2,1,0:T(8,128)S(1)}, f32[36,32,256]{2,1,0:T(8,128)}, u32[]{:S(2)}) copy-start(f32[36,32,256]{2,1,0:T(8,128)} %param.6) | copy-start | bytes 3538948
  12.5 12.4 %all-to-all-start.1 = ((s32[4,8,6]{2,0,1:T(4,128)}), s32[4,8,6]{2,0,1:T(4,128)S(1)}, u32[]{:S(2)}, u32[]{:S(2)}) async-start(s32[4,8,6]{2,0,1:T(4,128)} %copy.24), calls=%async_computation.1 | async-start | bytes 32768 | tf_op jit(solution)/shard_map/all_to_all | solution.py:32
  52.1 3.5 %copy-start.2 = (bf16[16,128]{1,0:T(8,128)(2,1)S(1)}, bf16[16,128]{1,0:T(8,128)(2,1)}, u32[]{:S(2)}) copy-start(bf16[16,128]{1,0:T(8,128)(2,1)} %param.11) | copy-start | bytes 12292
  52.1 3.6 %copy-start = (bf16[16,128,1024]{2,1,0:T(8,128)(2,1)S(1)}, bf16[16,128,1024]{2,1,0:T(8,128)(2,1)}, u32[]{:S(2)}) copy-start(bf16[16,128,1024]{2,1,0:T(8,128)(2,1)} %param.8) | copy-start | bytes 12582916
  73.5 23.6 %all-to-all-start.5 = ((f32[4,8,6,1024]{3,0,2,1:T(4,128)}), f32[4,8,6,1024]{3,0,2,1:T(4,128)S(1)}, u32[]{:S(2)}, u32[]{:S(2)}) async-start(f32[4,8,6,1024]{3,0,2,1:T(4,128)} %copy.33), calls=%async_computation.5 | async-start | bytes 1572864 | tf_op jit(solution)/shard_map/all_to_all | solution.py:62
where the time goes:
time: 105 us
  blocking collectives  46.1 us (44%)
  waiting for transfers between devices  26.1 us (25%)
  local copies, waits for them, and re-layouts  10.5 us (10%)
  starting transfers between devices  9.38 us (9%)
  other arithmetic  8.13 us (8%)
  matrix products  4.17 us (4%)
    all_to_all x1, waiting for transfers between devices, local(): lax.all_to_all(lax.all_to_all(back_buffer, 'slab', split_axis=0, concat_a...  19.9 us
    all_to_all x1, blocking collectives, local(): lax.all_to_all(lax.all_to_all(served_requests, 'slab', split_axis=0, conc...  14.4 us
    all_to_all x1, blocking collectives, local(): lax.all_to_all(back_buffer, 'slab', split_axis=0, concat_axis=0, tiled=True)  14 us
    all_to_all x1, blocking collectives, local(): lax.all_to_all(served_requests, 'slab', split_axis=0, concat_axis=0, tile...  9.8 us
    all_to_all x1, blocking collectives, local(): lax.all_to_all(id_buffer, 'slab', split_axis=0, concat_axis=0, tiled=True)  7.9 us
    all_to_all x1, waiting for transfers between devices, local(): lax.all_to_all(lax.all_to_all(id_buffer, 'slab', split_axis=0, concat_axi...  6.12 us
    all_to_all x1, starting transfers between devices, local(): lax.all_to_all(lax.all_to_all(id_buffer, 'slab', split_axis=0, concat_axi...  5.83 us
    all_to_all x1, starting transfers between devices, local(): lax.all_to_all(lax.all_to_all(back_buffer, 'slab', split_axis=0, concat_a...  3.55 us
  transfers between devices with their start and end apart: 2, of which 2 were waited for; matrix products, arithmetic and copies ran while one was open for 1% of the time, Pallas kernels for 0%

commit v1 on v0

--- a/solution.py
+++ b/solution.py
@@ -59,12 +59,20 @@
         .at[destination, owner_rep, position_order]
         .set(own_back)
     )
-    received_tiles = lax.all_to_all(
-        lax.all_to_all(back_buffer, "slab", split_axis=0, concat_axis=0, tiled=True),
-        "rep",
-        split_axis=1,
-        concat_axis=1,
-        tiled=True,
+    received_tiles = jnp.concatenate(
+        lax.all_to_all(
+            jnp.stack(
+                jnp.split(
+                    lax.all_to_all(back_buffer, "slab", split_axis=0, concat_axis=0, tiled=True),
+                    lax.axis_size("rep"),
+                    axis=1,
+                )
+            ),
+            "rep",
+            0,
+            0,
+        ),
+        axis=1,
     )
     owned = (
         jnp.zeros(local_blocks.shape, jnp.float32)

time: 105 us -> 109 us (1.038)
  local copies, waits for them, and re-layouts: 10.5 us -> 14.6 us
    unnamed x6 -> x13, local copies, waits for them, and re-layouts: 0.02 us -> 5.07 us
    all_to_all x2 -> x0, local copies, waits for them, and re-layouts: 1.86 us -> none  [the longest x1 1.39 us: local(): lax.all_to_all(back_buffer, 'slab', split_axis=0, concat_axis=0, tiled=True)]
    another operation x1 -> x3, local copies, waits for them, and re-layouts: 0.01 us -> 1.72 us  [the longest x1 0.99 us: local(): received_tiles.reshape(-1, width)]
where the time goes in v1:
time: 109 us
  blocking collectives  46.1 us (42%)
  waiting for transfers between devices  26.1 us (24%)
  local copies, waits for them, and re-layouts  14.6 us (13%)
  starting transfers between devices  9.38 us (9%)
  other arithmetic  8.13 us (7%)
  matrix products  4.17 us (4%)
    all_to_all x1, waiting for transfers between devices, local(): lax.all_to_all(jnp.stack(jnp.split(lax.all_to_all(back_buffer, 'slab', sp...  19.9 us
    all_to_all x1, blocking collectives, local(): lax.all_to_all(lax.all_to_all(served_requests, 'slab', split_axis=0, conc...  14.4 us
    all_to_all x1, blocking collectives, local(): lax.all_to_all(back_buffer, 'slab', split_axis=0, concat_axis=0, tiled=True)  14 us
    all_to_all x1, blocking collectives, local(): lax.all_to_all(served_requests, 'slab', split_axis=0, concat_axis=0, tile...  9.8 us
    all_to_all x1, blocking collectives, local(): lax.all_to_all(id_buffer, 'slab', split_axis=0, concat_axis=0, tiled=True)  7.9 us
    all_to_all x1, waiting for transfers between devices, local(): lax.all_to_all(lax.all_to_all(id_buffer, 'slab', split_axis=0, concat_axi...  6.12 us
    all_to_all x1, starting transfers between devices, local(): lax.all_to_all(lax.all_to_all(id_buffer, 'slab', split_axis=0, concat_axi...  5.83 us
    unnamed x13, local copies, waits for them, and re-layouts  5.07 us
  transfers between devices with their start and end apart: 2, of which 2 were waited for; matrix products, arithmetic and copies ran while one was open for 1% of the time, Pallas kernels for 0%

profile of v1, /device:TPU:0, one launch (start us, length us, event | category | flops | bytes accessed | tf_op | source)
XLA Modules:
  0.0 108.7 jit_solution(15524404668381821218)
XLA Ops:
  0.0 0.8 fusion.16
  0.8 0.7 bitcast_add_fusion
  1.7 0.7 fusion.20
  2.4 1.5 %scatter_fusion = s32[4,8,6]{1,0,2:T(4,128)S(1)} fusion(s32[4,8,6]{1,0,2:T(4,128)S(1)} %broadcast.74, s32[16]{0:T(128)S(1)} %get-tuple-element.8, s32[16]{0:T(128)S(1)} %get-tuple-element.5), kind=kCustom, calls=%fused_computation.2 | custom fusion | bytes 384 | tf_op jit(solution)/shard_map/scatter | solution.py:30
  3.9 7.9 %all_to_all.30 = s32[4,8,6]{1,2,0:T(8,128)S(1)} all-to-all(s32[4,8,6]{1,2,0:T(8,128)S(1)} %copy.22), channel_id=1, replica_groups=mesh['slab'=4,'rep'=8] {'slab'}, dimensions={0} | all-to-all | bytes 1536 | tf_op jit(solution)/shard_map/all_to_all | solution.py:33
  11.8 0.7 copy.23
  12.5 5.8 %all-to-all-start.1 = ((s32[4,8,6]{2,0,1:T(4,128)}), s32[4,8,6]{2,0,1:T(4,128)S(1)}, u32[]{:S(2)}, u32[]{:S(2)}) async-start(s32[4,8,6]{2,0,1:T(4,128)} %copy.23), calls=%async_computation.1 | async-start | bytes 32768 | tf_op jit(solution)/shard_map/all_to_all | solution.py:32
  18.5 0.4 reshape.57
  18.8 6.1 %all-to-all-done.1 = s32[4,8,6]{2,0,1:T(4,128)S(1)} async-done(((s32[4,8,6]{2,0,1:T(4,128)}), s32[4,8,6]{2,0,1:T(4,128)S(1)}, u32[]{:S(2)}, u32[]{:S(2)}) %all-to-all-start.1) | async-done | bytes 800 | tf_op jit(solution)/shard_map/all_to_all | solution.py:32
  25.3 1.0 gather_fusion
  26.7 9.8 %all_to_all.31 = bf16[4,8,6,1024]{3,1,2,0:T(8,128)(2,1)S(1)} all-to-all(bf16[4,8,6,1024]{3,1,2,0:T(8,128)(2,1)S(1)} %copy.29), channel_id=1, replica_groups=mesh['slab'=4,'rep'=8] {'slab'}, dimensions={0} | all-to-all | bytes 786432 | tf_op jit(solution)/shard_map/all_to_all | solution.py:41
  36.5 0.3 copy.30
  36.8 14.4 %all_to_all.32 = bf16[4,8,6,1024]{3,0,2,1:T(4,128)(2,1)S(1)} all-to-all(bf16[4,8,6,1024]{3,0,2,1:T(4,128)(2,1)S(1)} %copy.30), channel_id=1, replica_groups=mesh['slab'=4,'rep'=8] {'rep'}, dimensions={1} | all-to-all | bytes 786432 | tf_op jit(solution)/shard_map/all_to_all | solution.py:40
  51.4 0.7 gather_fusion.1
  52.1 3.5 %fusion.10 = f32[16,1,128]{2,1,0:T(1,128)S(1)} fusion(bf16[16,128,1024]{2,1,0:T(8,128)(2,1)} %param.8, bf16[16,1024,1]{1,0,2:T(8,128)(2,1)S(1)} %bitcast.68), kind=kOutput, calls=%fused_computation.25 | convolution fusion | flops 4194304 | bytes 4235264 | tf_op jit(solution)/shard_map/tev,tv->te/dot_general | solution.py:48
  55.7 0.7 fusion.12
  56.4 1.6 %scatter_fusion.1 = f32[4,8,6,1024]{3,1,2,0:T(8,128)S(1)} fusion(f32[4,8,6,1024]{3,1,2,0:T(8,128)S(1)} %broadcast_in_dim.10, s32[16]{0:T(128)S(1)} %get-tuple-element.8, f32[16,1024]{1,0:T(8,128)S(1)} %bitcast.69), kind=kCustom, calls=%fused_computation.3 | custom fusion | bytes 196800 | tf_op jit(solution)/shard_map/scatter | solution.py:60
  58.0 14.0 %all_to_all.33 = f32[4,8,6,1024]{3,1,2,0:T(8,128)S(1)} all-to-all(f32[4,8,6,1024]{3,1,2,0:T(8,128)S(1)} %scatter_fusion.1), channel_id=1, replica_groups=mesh['slab'=4,'rep'=8] {'slab'}, dimensions={0} | all-to-all | bytes 1572864 | tf_op jit(solution)/shard_map/all_to_all | solution.py:66
  72.1 0.7 fusion.9
  72.8 0.7 fusion.8
  73.5 0.7 fusion.7
  74.2 0.7 fusion.6
  75.0 0.7 fusion.5
  75.7 0.7 fusion.4
  76.4 0.7 fusion.3
  77.1 0.7 fusion.2
  77.9 3.5 %all-to-all-start.5 = ((f32[8,4,1,6,1024]{4,2,3,1,0:T(1,128)}), f32[8,4,1,6,1024]{4,2,3,1,0:T(1,128)S(1)}, u32[]{:S(2)}, u32[]{:S(2)}) async-start(f32[8,4,1,6,1024]{4,2,3,1,0:T(1,128)} %fusion.2), calls=%async_computation.5 | async-start | bytes 1572864 | tf_op jit(solution)/shard_map/all_to_all | solution.py:63
  81.6 19.9 %all-to-all-done.5 = f32[8,4,1,6,1024]{4,2,3,1,0:T(1,128)S(1)} async-done(((f32[8,4,1,6,1024]{4,2,3,1,0:T(1,128)}), f32[8,4,1,6,1024]{4,2,3,1,0:T(1,128)S(1)}, u32[]{:S(2)}, u32[]{:S(2)}) %all-to-all-start.5) | async-done | bytes 786464 | tf_op jit(solution)/shard_map/all_to_all | solution.py:63
  101.7 1.0 reshape.90
  102.7 3.0 %scatter_custom_fusion.2 = f32[288,1024]{1,0:T(8,128)S(1)} fusion(s32[192]{0:T(256)S(1)} %bitcast.72, f32[192,1024]{1,0:T(8,128)} %reshape.90, f32[]{:T(128)} %constant.55.clone.1), kind=kCustom, calls=%fused_computation.6 | custom fusion | flops 196608 | bytes 1180160 | tf_op jit(solution)/shard_map/scatter-add | solution.py:80
  105.7 0.3 reshape.59
  106.0 2.6 %multiply_divide_fusion = f32[36,32,256]{2,1,0:T(8,128)} fusion(f32[36,32,256]{2,1,0:T(8,128)} %param.7, f32[36,32,256]{2,1,0:T(8,128)S(1)} %copy-done.1, f32[36,32,256]{2,1,0:T(8,128)S(1)} %reshape.59), kind=kLoop, calls=%fused_computation.5 | loop fusion | flops 589824 | bytes 4718592 | tf_op jit(solution)/shard_map/div | solution.py:82
  (27 shorter events, 1.7 us)
Async XLA Ops:
  0.0 18.4 %copy-start.1 = (f32[36,32,256]{2,1,0:T(8,128)S(1)}, f32[36,32,256]{2,1,0:T(8,128)}, u32[]{:S(2)}) copy-start(f32[36,32,256]{2,1,0:T(8,128)} %param.6) | copy-start | bytes 3538948
  12.5 12.4 %all-to-all-start.1 = ((s32[4,8,6]{2,0,1:T(4,128)}), s32[4,8,6]{2,0,1:T(4,128)S(1)}, u32[]{:S(2)}, u32[]{:S(2)}) async-start(s32[4,8,6]{2,0,1:T(4,128)} %copy.23), calls=%async_computation.1 | async-start | bytes 32768 | tf_op jit(solution)/shard_map/all_to_all | solution.py:32
  52.1 3.5 %copy-start.2 = (bf16[16,128]{1,0:T(8,128)(2,1)S(1)}, bf16[16,128]{1,0:T(8,128)(2,1)}, u32[]{:S(2)}) copy-start(bf16[16,128]{1,0:T(8,128)(2,1)} %param.11) | copy-start | bytes 12292
  52.1 3.6 %copy-start = (bf16[16,128,1024]{2,1,0:T(8,128)(2,1)S(1)}, bf16[16,128,1024]{2,1,0:T(8,128)(2,1)}, u32[]{:S(2)}) copy-start(bf16[16,128,1024]{2,1,0:T(8,128)(2,1)} %param.8) | copy-start | bytes 12582916
  77.9 23.6 %all-to-all-start.5 = ((f32[8,4,1,6,1024]{4,2,3,1,0:T(1,128)}), f32[8,4,1,6,1024]{4,2,3,1,0:T(1,128)S(1)}, u32[]{:S(2)}, u32[]{:S(2)}) async-start(f32[8,4,1,6,1024]{4,2,3,1,0:T(1,128)} %fusion.2), calls=%async_computation.5 | async-start | bytes 1572864 | tf_op jit(solution)/shard_map/all_to_all | solution.py:63
